TPU v7x, 32 devices: a whole 2x2x4 slice. The times are simulated.
32 devices in a mesh: gx: 4 (over z), gy: 2 (over x), gz: 4 (over y, core).
Axes of the slice: x: 2, y: 2, z: 4, core: 2. Of those that a mesh axis runs over, the one named last changes fastest.
Arguments:
- right_side: float32 [4, 2, 8, 128], P('gx', 'gy', 'gz'), may hold values from -8 to 8
- diag_blocks: float32 [4, 2, 8, 128, 128], P('gx', 'gy', 'gz'), may hold values from -0.035 to 2.04, as said below
- couplings: float32 [3, 4, 2, 8, 128, 128], P(None, 'gx', 'gy', 'gz'), may hold values from -0.04 to 0.04
- pattern: int32 [3, 4, 2, 8], P(None, 'gx', 'gy', 'gz'), may hold values 0 or 1
- deflation: float32 [4, 2, 8, 32, 128], P('gx', 'gy', 'gz'), may hold values from -5 to 5
Outputs:
- solution: float32 [4, 2, 8, 128], P('gx', 'gy', 'gz')
- residual: float32 [4, 2, 8, 128], P('gx', 'gy', 'gz')
Inputs may be any that keep to these rules, and one draw needn't show every extreme that they name: `diag_blocks`: each diagonal block is symmetric.
All inputs are finite; a program needn't handle non-finite values. No bound on the sum of `pattern` on one device may be relied on, other than what follows from the above.
Results may differ from a plain program's by a relative error of at most 0.00035.
Values sent between devices are 32-bit elements; how exact they have to be, the bound alone decides.
A program may use at most 64 MiB of HBM per device.

v0:
```python
import functools
import math

import jax
import jax.numpy as jnp
from jax import lax
from jax.experimental import pallas as pl
from jax.experimental.pallas import tpu as pltpu
from jax.sharding import PartitionSpec as P

ITERS = 3
AXES = ("gx", "gy", "gz")
COARSE_GROUPS = (("gy", "gz"), ("gx",))
UNROLLED = 32
DOT_GROUPS = (("gx", "gy", "gz"),)
MESH = pl.DeviceIdType.MESH
F32 = jnp.float32
BF16 = jnp.bfloat16


def place(index, group, sizes):
    coords = {}
    for axis in reversed(group):
        coords[axis] = lax.rem(index, sizes[axis])
        index = lax.div(index, sizes[axis])
    return coords


def position(group, sizes):
    index = 0
    for axis in group:
        index = index * sizes[axis] + lax.axis_index(axis)
    return index


def extent(group, sizes):
    return math.prod(sizes[axis] for axis in group)


def for_peers(group, sizes, action):
    count = extent(group, sizes)
    me = position(group, sizes)

    def body(k, carry):
        action(place(lax.rem(me + k, count), group, sizes))
        return carry

    if count <= UNROLLED:
        for k in range(1, count):
            body(k, 0)
    else:
        lax.fori_loop(1, count, body, 0)


def split_rows(v):
    high = v.astype(BF16).astype(F32)
    rest = v - high
    middle = rest.astype(BF16).astype(F32)
    low = rest - middle
    if v.shape[0] == 1:
        row = lax.broadcasted_iota(jnp.int32, (8, v.shape[1]), 0)
        parts = jnp.where(row == 0, high, jnp.where(row == 1, middle, jnp.where(row == 2, low, 0.0)))
    else:
        parts = jnp.concatenate([high, middle, low], axis=0)
    return parts.astype(BF16)


def join_rows(out, rows):
    return out[:rows] + (out[rows : 2 * rows] + out[2 * rows : 3 * rows])


def split_pair(m):
    high = m.astype(BF16)
    return high, (m - high.astype(F32)).astype(BF16)


def times(v, high, low):
    parts = split_rows(v)
    out = jnp.dot(parts, high, preferred_element_type=F32)
    out = out + jnp.dot(parts, low, preferred_element_type=F32)
    return join_rows(out, v.shape[0])


def times_t(v, high, low):
    parts = split_rows(v)
    dims = (((1,), (1,)), ((), ()))
    out = lax.dot_general(parts, high, dims, preferred_element_type=F32)
    out = out + lax.dot_general(parts, low, dims, preferred_element_type=F32)
    return join_rows(out, v.shape[0])


def kernel(sizes, lz, block, defl, *refs):
    inputs = refs[:5]
    sol_ref, res_ref = refs[5:7]
    (loc_h, loc_l, out_h, out_l, in_h, in_l, zo_h, zo_l, zi_h, zi_l, proj_h, proj_l) = refs[7:19]
    n_ops = 1 + ITERS
    at = 19
    ops = []
    for _ in range(n_ops):
        ops.append(refs[at : at + 9])
        at += 9
    coarse_bufs = refs[at : at + len(COARSE_GROUPS)]
    at += len(COARSE_GROUPS)
    moment_bufs = refs[at : at + len(COARSE_GROUPS)]
    at += len(COARSE_GROUPS)
    dot_bufs = [refs[at + k * len(DOT_GROUPS) : at + (k + 1) * len(DOT_GROUPS)] for k in range(ITERS - 1)]
    at += (ITERS - 1) * len(DOT_GROUPS)
    halo_send, halo_recv, red_send, red_recv, load_sem = refs[at : at + 5]
    staged = refs[at + 5 : at + 10]
    loads = [pltpu.make_async_copy(src, dst, load_sem.at[k]) for k, (src, dst) in enumerate(zip(inputs, staged))]
    for load in loads:
        load.start()
    right_ref, diag_ref, coup_ref, pat_ref, defl_ref = staged

    idx = {axis: lax.axis_index(axis) for axis in AXES}
    lower = {axis: idx[axis] > 0 for axis in AXES}
    upper = {axis: idx[axis] < sizes[axis] - 1 for axis in AXES}
    barrier = pltpu.get_barrier_semaphore()

    for op in ops:
        for ref in op[4:9]:
            ref[...] = jnp.zeros_like(ref)
        op[3][...] = jnp.zeros_like(op[3])

    def greet(peer):
        pl.semaphore_signal(barrier, inc=1, device_id=peer, device_id_type=MESH)

    for group in COARSE_GROUPS:
        for_peers(group, sizes, greet)
    for load in loads:
        load.wait()

    def gate(d, c):
        return pat_ref[0, 0, c : c + 1, d : d + 1].astype(F32)

    def put(ref_h, ref_l, rows, cols, value):
        high, low = split_pair(value)
        ref_h[rows, cols] = high
        ref_l[rows, cols] = low

    def span(c):
        return slice(c * block, (c + 1) * block)

    if lz > 2:
        loc_h[...] = jnp.zeros_like(loc_h)
        loc_l[...] = jnp.zeros_like(loc_l)
    for c in range(lz):
        put(loc_h, loc_l, span(c), span(c), diag_ref[0, 0, c])
        cx = gate(0, c) * coup_ref[0, 0, 0, c]
        cy = gate(1, c) * coup_ref[1, 0, 0, c]
        cz = gate(2, c) * coup_ref[2, 0, 0, c]
        put(out_h.at[c], out_l.at[c], slice(None), span(0), cx)
        put(out_h.at[c], out_l.at[c], slice(None), span(1), cy)
        put(in_h.at[c], in_l.at[c], span(0), slice(None), cx.T)
        put(in_h.at[c], in_l.at[c], span(1), slice(None), cy.T)
        if c + 1 < lz:
            put(loc_h, loc_l, span(c), span(c + 1), cz)
            put(loc_h, loc_l, span(c + 1), span(c), cz.T)
        else:
            put(zo_h, zo_l, slice(None), slice(None), cz)
            put(zi_h, zi_l, slice(None), slice(None), cz.T)

    right = jnp.concatenate([right_ref[0, 0, c : c + 1, :] for c in range(lz)], axis=1)
    basis = jnp.concatenate([defl_ref[0, 0, c] for c in range(lz)], axis=1)

    def halo_copies(k):
        field, car_x, car_y, car_z, bey_x, bey_y, bey_z, arr_xy, arr_z = ops[k]
        routes = (
            ("gx", -1, field, bey_x),
            ("gy", -1, field, bey_y),
            ("gz", -1, field.at[0], bey_z),
            ("gx", 1, car_x, arr_xy.at[0]),
            ("gy", 1, car_y, arr_xy.at[1]),
            ("gz", 1, car_z, arr_z),
        )
        copies = []
        for j, (axis, way, src, dst) in enumerate(routes):
            copies.append(
                (
                    lower[axis] if way < 0 else upper[axis],
                    upper[axis] if way < 0 else lower[axis],
                    pltpu.make_async_remote_copy(
                        src_ref=src,
                        dst_ref=dst,
                        send_sem=halo_send.at[k, j],
                        recv_sem=halo_recv.at[k, j],
                        device_id={axis: jnp.clip(idx[axis] + way, 0, sizes[axis] - 1)},
                        device_id_type=MESH,
                    ),
                )
            )
        return copies

    def start(copies):
        for sends, _, copy in copies:
            pl.when(sends)(copy.start)

    def open_product(k, v, later=None):
        field, car_x, car_y, car_z = ops[k][:4]
        copies = halo_copies(k) if later is None else None
        for c in range(lz):
            field[c] = v[:, span(c)]
        if later is None:
            start(copies[:3])
        for c in range(lz):
            carried = times(v[:, span(c)], out_h[c], out_l[c])
            car_x[c] = carried[:, span(0)]
            car_y[c] = carried[:, span(1)]
        car_z[...] = times(v[:, span(lz - 1)], zo_h[...], zo_l[...])
        if later is None:
            start(copies[3:])
        return times(v, loc_h[...], loc_l[...])

    def close_product(k, own):
        _, _, _, _, bey_x, bey_y, bey_z, arr_xy, arr_z = ops[k]
        for _, comes, copy in halo_copies(k):
            pl.when(comes)(copy.wait_recv)
        parts = []
        for c in range(lz):
            beyond = jnp.concatenate([bey_x[c], bey_y[c]], axis=1)
            part = times(beyond, in_h[c], in_l[c])
            part = part + arr_xy[0, c] + arr_xy[1, c]
            if c == 0:
                part = part + arr_z[...]
            if c == lz - 1:
                part = part + times(bey_z[...], zi_h[...], zi_l[...])
            parts.append(part)
        return own + jnp.concatenate(parts, axis=1)

    def gathered(buf, sem):
        rest = buf.at[pl.ds(0, buf.shape[0] - 1)]
        return pltpu.make_async_copy(rest, rest, sem)

    def reduce_start(buf, group, sem, value):
        me = position(group, sizes)
        buf[me] = value
        own = buf.at[me]

        def send(peer):
            pltpu.make_async_remote_copy(
                src_ref=own,
                dst_ref=own,
                send_sem=red_send.at[sem],
                recv_sem=red_recv.at[sem],
                device_id=peer,
                device_id_type=MESH,
            ).start()

        for_peers(group, sizes, send)

    def reduce_done(buf, sem):
        gathered(buf, red_recv.at[sem]).wait()
        return jnp.sum(buf[...], axis=0)

    def spread(coef, fields):
        return jnp.sum(coef * fields, axis=0, keepdims=True)

    rows_first = ops[0][0].shape[1]
    first = jnp.concatenate([basis, right, jnp.zeros((rows_first - defl - 1, lz * block), F32)], axis=0)
    pl.semaphore_wait(barrier, sum(extent(group, sizes) - 1 for group in COARSE_GROUPS))
    own = open_product(0, first)
    proj_h[...] = jnp.zeros_like(proj_h)
    proj_l[...] = jnp.zeros_like(proj_l)
    everything = slice(None)
    put(proj_h, proj_l, slice(0, defl), everything, basis)
    right_local = times_t(right, proj_h[...], proj_l[...])
    both = close_product(0, own)
    applied = both[:defl]
    image = both[defl : defl + 1]

    reps = block // defl
    apart = defl // reps
    for g in range(reps):
        put(proj_h, proj_l, slice(g * defl, (g + 1) * defl), everything, applied)
    coarse_local = times_t(basis, proj_h[...], proj_l[...])
    lane = lax.broadcasted_iota(jnp.int32, (apart, block), 1)
    lane_row = lax.broadcasted_iota(jnp.int32, (1, block), 1)
    col = lax.broadcasted_iota(jnp.int32, (defl, block), 1)
    row = lax.broadcasted_iota(jnp.int32, (defl, block), 0)
    eye = jnp.where(row == col, 1.0, 0.0)

    def pack(repeated):
        packed = jnp.zeros((apart, block), F32)
        for g in range(reps):
            inside = (lane >= g * defl) & (lane < (g + 1) * defl)
            packed = packed + jnp.where(inside, repeated[g * apart : (g + 1) * apart], 0.0)
        return packed

    def unpack(packed):
        groups = [packed] + [pltpu.roll(packed, block - g * defl, 1) for g in range(1, reps)]
        return jnp.where(col < defl, jnp.concatenate(groups, axis=0), 0.0)

    def on_applied(v):
        return times_t(v, proj_h[...], proj_l[...])

    stages = len(COARSE_GROUPS)
    value = jnp.concatenate([pack(coarse_local), jnp.broadcast_to(right_local, (8, block))], axis=0)
    reduce_start(coarse_bufs[0], COARSE_GROUPS[0], 0, value)
    own = open_product(1, both)
    second = pack(on_applied(applied))
    h_right, h_image = on_applied(right), on_applied(image)
    sq = jnp.sum(right * right, axis=1, keepdims=True)
    cross = jnp.sum(right * image, axis=1, keepdims=True)
    h_right = jnp.where(lane_row == defl, sq, jnp.where(lane_row == defl + 1, cross, h_right))
    row8 = lax.broadcasted_iota(jnp.int32, (8, block), 0)
    vectors = jnp.where(row8 == 0, h_right, h_image)
    for k in range(1, stages):
        value = reduce_done(coarse_bufs[k - 1], k - 1)
        reduce_start(coarse_bufs[k], COARSE_GROUPS[k], k, value)
    both_twice = close_product(1, own)
    twice = both_twice[:defl]
    image_twice = both_twice[defl : defl + 1]
    moments = jnp.concatenate([second, pack(on_applied(twice)), vectors], axis=0)
    reduce_start(moment_bufs[0], COARSE_GROUPS[0], stages, moments)
    own = open_product(2, twice, "later")
    value = reduce_done(coarse_bufs[-1], stages - 1)
    coarse = unpack(value[:apart])
    square = jnp.concatenate([coarse, jnp.zeros((block - defl, block), F32)], axis=0)
    inv = 0.5 * (coarse + square.T[:defl])
    for k in range(defl):
        if k == defl // 2:
            for j in range(1, stages):
                moments = reduce_done(moment_bufs[j - 1], stages + j - 1)
                reduce_start(moment_bufs[j], COARSE_GROUPS[j], stages + j, moments)
            start(halo_copies(2))
        pivot = 1.0 / inv[k : k + 1, k : k + 1]
        line = jnp.where(col[:1] == k, pivot, inv[k : k + 1] * pivot)
        inv = jnp.where(row == k, line, jnp.where(col == k, 0.0, inv) - inv[:, k : k + 1] * line)

    def coarse_solve(projected):
        return jnp.sum(inv * projected, axis=1, keepdims=True)

    coef = coarse_solve(value[apart : apart + 1])
    coef_row = spread(coef, eye)
    x = spread(coef, basis)
    r = right - spread(coef, applied)
    w = image - spread(coef, twice)
    moments = reduce_done(moment_bufs[-1], 2 * stages - 1)
    h_right = moments[2 * apart : 2 * apart + 1]
    h_image = moments[2 * apart + 1 : 2 * apart + 2]
    onto = spread(coef, unpack(moments[:apart]))
    onto_image = spread(coef, unpack(moments[apart : 2 * apart]))
    sq = h_right[:, defl : defl + 1] + jnp.sum(coef_row * (onto - 2.0 * h_right), axis=1, keepdims=True)
    cross = h_right[:, defl + 1 : defl + 2] + jnp.sum(coef_row * (onto_image - 2.0 * h_image), axis=1, keepdims=True)
    total = jnp.where(lane_row == defl, sq, jnp.where(lane_row == defl + 1, cross, h_right - onto))
    q = image_twice - spread(coef, close_product(2, own))
    d = s = z = curv = norm = None
    sem = 2 * stages
    for it in range(ITERS):
        last = it + 1 == ITERS
        if it > 0:
            local = on_applied(r)
            sq = jnp.sum(r * r, axis=1, keepdims=True)
            cross = jnp.sum(r * w, axis=1, keepdims=True)
            local = jnp.where(lane_row == defl, sq, jnp.where(lane_row == defl + 1, cross, local))
            bufs = dot_bufs[it - 1]
            reduce_start(bufs[0], DOT_GROUPS[0], sem, local)
            if not last:
                own = open_product(2 + it, w)
            for k in range(1, len(DOT_GROUPS)):
                local = reduce_done(bufs[k - 1], sem)
                sem += 1
                reduce_start(bufs[k], DOT_GROUPS[k], sem, local)
            if not last:
                q = close_product(2 + it, own)
            total = reduce_done(bufs[-1], sem)
            sem += 1
        coef = coarse_solve(total)
        mine = jnp.sum(eye * total, axis=1, keepdims=True)
        energy = jnp.sum(mine * coef, axis=0, keepdims=True)
        norm_new = total[:, defl : defl + 1]
        cross = total[:, defl + 1 : defl + 2]
        if it == 0:
            d = r - spread(coef, basis)
            s = w - spread(coef, applied)
            z = q - spread(coef, twice)
            curv = cross - energy
        else:
            growth = norm_new / norm
            d = r + growth * d - spread(coef, basis)
            s = w + growth * s - spread(coef, applied)
            if not last:
                z = q + growth * z - spread(coef, twice)
            curv = cross - growth * growth * curv - energy
        norm = norm_new
        step = norm / curv
        x = x + step * d
        r = r - step * s
        if not last:
            w = w - step * z
    for c in range(lz):
        sol_ref[0, 0, c : c + 1, :] = x[:, span(c)]
        res_ref[0, 0, c : c + 1, :] = r[:, span(c)]

    for k in range(n_ops):
        for sends, _, copy in halo_copies(k):
            pl.when(sends)(copy.wait_send)
    every = list(coarse_bufs) + list(moment_bufs) + [buf for bufs in dot_bufs for buf in bufs]
    for k, buf in enumerate(every):
        gathered(buf, red_send.at[k]).wait()


def hand_out(sol_ref, res_ref, sol_out, res_out, sol_held, res_held, sems):
    def move(routes, k):
        copies = [pltpu.make_async_copy(src, dst, sems.at[k, j]) for j, (src, dst) in enumerate(routes)]
        for copy in copies:
            copy.start()
        for copy in copies:
            copy.wait()

    move(((sol_ref, sol_held), (res_ref, res_held)), 0)
    move(((sol_held, sol_out), (res_held, res_out)), 1)


def solution(mesh):
    sizes = dict(mesh.shape)
    in_specs = (
        P("gx", "gy", "gz", None),
        P("gx", "gy", "gz", None, None),
        P(None, "gx", "gy", "gz", None, None),
        P(None, "gx", "gy", "gz"),
        P("gx", "gy", "gz", None, None),
    )
    out_specs = (P("gx", "gy", "gz", None), P("gx", "gy", "gz", None))

    def per_device(right_side, diag_blocks, couplings, pattern, deflation):
        lx, ly, lz, block = right_side.shape
        pattern = jnp.transpose(pattern, (1, 2, 3, 0))
        assert lx == 1 and ly == 1
        defl = deflation.shape[3]
        rows_first = (defl + 1 + 7) // 8 * 8
        wide = lz * block
        scratch = []
        for shape in (
            (wide, wide),
            (lz, block, 2 * block),
            (lz, 2 * block, block),
            (block, block),
            (block, block),
            (block, wide),
        ):
            scratch += [pltpu.VMEM(shape, BF16)] * 2
        for rows in (rows_first, rows_first, defl) + (1,) * (ITERS - 2):
            layer, face = (lz, rows, block), (rows, block)
            scratch += [pltpu.VMEM(layer, F32)] * 3 + [pltpu.VMEM(face, F32)]
            scratch += [pltpu.VMEM(layer, F32)] * 2 + [pltpu.VMEM(face, F32)]
            scratch += [pltpu.VMEM((2,) + layer, F32), pltpu.VMEM(face, F32)]
        for group in COARSE_GROUPS:
            scratch.append(pltpu.VMEM((extent(group, sizes), defl * defl // block + 8, block), F32))
        for group in COARSE_GROUPS:
            scratch.append(pltpu.VMEM((extent(group, sizes), 2 * defl * defl // block + 8, block), F32))
        for _ in range(ITERS - 1):
            for group in DOT_GROUPS:
                scratch.append(pltpu.VMEM((extent(group, sizes), 1, block), F32))
        reductions = 2 * len(COARSE_GROUPS) + (ITERS - 1) * len(DOT_GROUPS)
        scratch += [pltpu.SemaphoreType.DMA((1 + ITERS, 6))] * 2
        scratch += [pltpu.SemaphoreType.DMA((reductions,))] * 2
        scratch.append(pltpu.SemaphoreType.DMA((5,)))
        for array in (right_side, diag_blocks, couplings, pattern, deflation):
            scratch.append(pltpu.VMEM(array.shape, array.dtype))
        vmem = pl.BlockSpec(memory_space=pltpu.VMEM)
        hbm = pl.BlockSpec(memory_space=pltpu.HBM)
        anywhere = pl.BlockSpec(memory_space=pl.ANY)
        out = jax.ShapeDtypeStruct(right_side.shape, F32)
        results = pl.pallas_call(
            functools.partial(kernel, sizes, lz, block, defl),
            out_shape=(out, out),
            in_specs=[hbm] * 5,
            out_specs=(vmem, vmem),
            scratch_shapes=scratch,
            compiler_params=pltpu.CompilerParams(
                collective_id=0, has_side_effects=True, vmem_limit_bytes=67_043_328
            ),
        )(right_side, diag_blocks, couplings, pattern, deflation)
        return pl.pallas_call(
            hand_out,
            out_shape=(out, out),
            in_specs=[anywhere, anywhere],
            out_specs=(hbm, hbm),
            scratch_shapes=[pltpu.VMEM(out.shape, F32)] * 2 + [pltpu.SemaphoreType.DMA((2, 2))],
            compiler_params=pltpu.CompilerParams(vmem_limit_bytes=67_043_328),
        )(*results)

    return jax.shard_map(
        per_device, mesh=mesh, in_specs=in_specs, out_specs=out_specs, check_vma=False
    )
```

profile of v0, /device:TPU:0, one launch (start us, length us, event | category | flops | bytes accessed | tf_op | source)
XLA Modules:
  0.0 36.1 jit_solution(6307193496858170776)
XLA Ops:
  0.6 34.2 %shard_map.68 = (f32[1,1,2,128]{3,2,1,0:T(2,128)}, f32[1,1,2,128]{3,2,1,0:T(2,128)}) custom-call(f32[1,1,2,128]{3,2,1,0:T(2,128)} %refs_0_.1, f32[1,1,2,128,128]{4,3,2,1,0:T(8,128)} %refs_1_.1, f32[3,1,1,2,128,128]{5,4,3,2,1,0:T(8,128)} %refs_2_.1, s32[1,1,2,3]{3,2,1,0:T(2,128)} %bitcast.1, f32[1,1,2,32,128]{4,3,2,1,0:T(8,128)} %refs_4_.1), custom_call_target="tpu_custom_call" | custom-call | tf_op jit(solution)/shard_map/pallas_call | solution.py:465
  34.8 1.3 %shard_map.69 = (f32[1,1,2,128]{3,2,1,0:T(2,128)}, f32[1,1,2,128]{3,2,1,0:T(2,128)}) custom-call(f32[1,1,2,128]{3,2,1,0:T(2,128)} %get-tuple-element.4.sol_ref, f32[1,1,2,128]{3,2,1,0:T(2,128)} %get-tuple-element.5.res_ref), custom_call_target="tpu_custom_call" | custom-call | tf_op jit(solution)/shard_map/pallas_call | solution.py:475
where the time goes:
time: 36.3 us; the launch traced here: 36.1 us
  Pallas kernels  35.5 us (98%)
  between operations  0.64 us (2%)
    pallas_call x1, Pallas kernels, per_device(): pl.pallas_call(functools.partial(kernel, sizes, lz, block, defl), out_sha...  34.2 us
    pallas_call x1, Pallas kernels, per_device(): pl.pallas_call(hand_out, out_shape=(out, out), in_specs=[anywhere, anywhe...  1.26 us

commit v1 on v0

v1 whole, which is shorter than its diff:
```python
import functools
import math

import jax
import jax.numpy as jnp
from jax import lax
from jax.experimental import pallas as pl
from jax.experimental.pallas import tpu as pltpu
from jax.sharding import PartitionSpec as P

ITERS = 3
AXES = ("gx", "gy", "gz")
COARSE_GROUPS = (("gy", "gz"), ("gx",))
UNROLLED = 32
LAST_GROUPS = (("gx", "gy", "gz"),)
DIRECT = 64
SHIFT = 1.45
GJ_FIRST = 10
MESH = pl.DeviceIdType.MESH
F32 = jnp.float32
BF16 = jnp.bfloat16


def place(index, group, sizes):
    coords = {}
    for axis in reversed(group):
        coords[axis] = lax.rem(index, sizes[axis])
        index = lax.div(index, sizes[axis])
    return coords


def position(group, sizes):
    index = 0
    for axis in group:
        index = index * sizes[axis] + lax.axis_index(axis)
    return index


def extent(group, sizes):
    return math.prod(sizes[axis] for axis in group)


def for_peers(group, sizes, action):
    count = extent(group, sizes)
    me = position(group, sizes)

    def body(k, carry):
        action(place(lax.rem(me + k, count), group, sizes))
        return carry

    if count <= UNROLLED:
        for k in range(1, count):
            body(k, 0)
    else:
        lax.fori_loop(1, count, body, 0)


def split_rows(v):
    high = v.astype(BF16).astype(F32)
    rest = v - high
    middle = rest.astype(BF16).astype(F32)
    low = rest - middle
    return jnp.concatenate([high, middle, low], axis=0).astype(BF16)


def join_rows(out, rows):
    return out[:rows] + (out[rows : 2 * rows] + out[2 * rows : 3 * rows])


def split_pair(m):
    high = m.astype(BF16)
    return high, (m - high.astype(F32)).astype(BF16)


def times(parts, high, low):
    out = jnp.dot(parts, high, preferred_element_type=F32)
    out = out + jnp.dot(parts, low, preferred_element_type=F32)
    return join_rows(out, parts.shape[0] // 3)


def times_t(parts, high, low):
    dims = (((1,), (1,)), ((), ()))
    out = lax.dot_general(parts, high, dims, preferred_element_type=F32)
    out = out + lax.dot_general(parts, low, dims, preferred_element_type=F32)
    return join_rows(out, parts.shape[0] // 3)


def last_groups(sizes):
    return LAST_GROUPS if extent(LAST_GROUPS[0], sizes) <= DIRECT else COARSE_GROUPS


def kernel(sizes, lz, block, defl, *refs):
    inputs = refs[:5]
    sol_ref, res_ref = refs[5:7]
    (loc_h, loc_l, out_h, out_l, in_h, in_l, zo_h, zo_l, zi_h, zi_l, proj_h, proj_l) = refs[7:19]
    n_ops = 1 + ITERS
    at = 19
    ops = []
    for _ in range(n_ops):
        ops.append(refs[at : at + 10])
        at += 10
    stages = len(COARSE_GROUPS)
    moment_bufs = [refs[at + j * stages : at + (j + 1) * stages] for j in range(ITERS)]
    at += ITERS * stages
    final_groups = last_groups(sizes)
    final_bufs = refs[at : at + len(final_groups)]
    at += len(final_groups)
    halo_send, halo_recv, red_send, red_recv, load_sem = refs[at : at + 5]
    staged = refs[at + 5 : at + 10]
    loads = [pltpu.make_async_copy(src, dst, load_sem.at[k]) for k, (src, dst) in enumerate(zip(inputs, staged))]
    for k in (0, 4, 3, 2, 1):
        loads[k].start()
    right_ref, diag_ref, coup_ref, pat_ref, defl_ref = staged

    idx = {axis: lax.axis_index(axis) for axis in AXES}
    lower = {axis: idx[axis] > 0 for axis in AXES}
    upper = {axis: idx[axis] < sizes[axis] - 1 for axis in AXES}
    barrier = pltpu.get_barrier_semaphore()

    def greet(peer):
        pl.semaphore_signal(barrier, inc=1, device_id=peer, device_id_type=MESH)

    for group in COARSE_GROUPS:
        for_peers(group, sizes, greet)

    def clear(axis, received, ways):
        @pl.when(jnp.logical_not(ways[axis]))
        def _():
            for op in ops:
                for ref in received(op):
                    ref[...] = jnp.zeros_like(ref)

    for j, axis in enumerate(AXES):
        clear(axis, lambda op: op[4 + j : 5 + j], upper)
        clear(axis, lambda op: op[7 + j : 8 + j], lower)

    rows = ops[0][0].shape[1]
    wide = lz * block

    def gate(d, c):
        return pat_ref[0, 0, c : c + 1, d : d + 1].astype(F32)

    def put(ref_h, ref_l, at_rows, at_cols, value):
        high, low = split_pair(value)
        ref_h[at_rows, at_cols] = high
        ref_l[at_rows, at_cols] = low

    def span(c):
        return slice(c * block, (c + 1) * block)

    def halo_copies(k, which=slice(None)):
        field, car_x, car_y, car_z, bey_x, bey_y, bey_z, arr_x, arr_y, arr_z = ops[k]
        routes = (
            ("gx", -1, field, bey_x),
            ("gy", -1, field, bey_y),
            ("gz", -1, field.at[0], bey_z),
            ("gx", 1, car_x, arr_x),
            ("gy", 1, car_y, arr_y),
            ("gz", 1, car_z, arr_z),
        )
        copies = []
        for j, (axis, way, src, dst) in list(enumerate(routes))[which]:
            copies.append(
                (
                    lower[axis] if way < 0 else upper[axis],
                    upper[axis] if way < 0 else lower[axis],
                    pltpu.make_async_remote_copy(
                        src_ref=src,
                        dst_ref=dst,
                        send_sem=halo_send.at[k, j],
                        recv_sem=halo_recv.at[k, j],
                        device_id={axis: jnp.clip(idx[axis] + way, 0, sizes[axis] - 1)},
                        device_id_type=MESH,
                    ),
                )
            )
        return copies

    def start(copies):
        for sends, _, copy in copies:
            pl.when(sends)(copy.start)

    def arrive(copies):
        for _, comes, copy in copies:
            pl.when(comes)(copy.wait_recv)

    def keep(k, v):
        field = ops[k][0]
        for c in range(lz):
            field[c] = v[:, span(c)]

    def carry(k, parts):
        _, car_x, car_y, car_z = ops[k][:4]
        for c in range(lz):
            carried = times(parts[:, span(c)], out_h[c], out_l[c])
            car_x[c] = carried[:, span(0)]
            car_y[c] = carried[:, span(1)]
        car_z[...] = times(parts[:, span(lz - 1)], zo_h[...], zo_l[...])

    def from_above(k):
        bey_x, bey_y, bey_z = ops[k][4:7]
        arrive(halo_copies(k, slice(0, 3)))
        out = []
        for c in range(lz):
            beyond = jnp.concatenate([bey_x[c], bey_y[c]], axis=1)
            part = times(split_rows(beyond), in_h[c], in_l[c])
            if c == lz - 1:
                part = part + times(split_rows(bey_z[...]), zi_h[...], zi_l[...])
            out.append(part)
        return jnp.concatenate(out, axis=1)

    def from_below(k):
        arr_x, arr_y, arr_z = ops[k][7:10]
        arrive(halo_copies(k, slice(3, 6)))
        out = []
        for c in range(lz):
            part = arr_x[c] + arr_y[c]
            if c == 0:
                part = part + arr_z[...]
            out.append(part)
        return jnp.concatenate(out, axis=1)

    def gathered(buf, sem):
        rest = buf.at[pl.ds(0, buf.shape[0] - 1)]
        return pltpu.make_async_copy(rest, rest, sem)

    def reduce_start(buf, group, sem, value):
        me = position(group, sizes)
        buf[me] = value
        own = buf.at[me]

        def send(peer):
            pltpu.make_async_remote_copy(
                src_ref=own,
                dst_ref=own,
                send_sem=red_send.at[sem],
                recv_sem=red_recv.at[sem],
                device_id=peer,
                device_id_type=MESH,
            ).start()

        for_peers(group, sizes, send)

    def reduce_done(buf, sem):
        gathered(buf, red_recv.at[sem]).wait()
        return jnp.sum(buf[...], axis=0)

    def moments_start(j, value):
        reduce_start(moment_bufs[j][0], COARSE_GROUPS[0], j * stages, value)

    def moments_next(j, stage):
        value = reduce_done(moment_bufs[j][stage - 1], j * stages + stage - 1)
        reduce_start(moment_bufs[j][stage], COARSE_GROUPS[stage], j * stages + stage, value)

    def moments_done(j):
        return reduce_done(moment_bufs[j][-1], (j + 1) * stages - 1)

    loads[0].wait()
    loads[4].wait()
    right = jnp.concatenate([right_ref[0, 0, c : c + 1, :] for c in range(lz)], axis=1)
    basis = jnp.concatenate([defl_ref[0, 0, c] for c in range(lz)], axis=1)
    first = jnp.concatenate([basis, right, jnp.zeros((rows - defl - 1, wide), F32)], axis=0)
    keep(0, first)
    first_parts = split_rows(first)
    loads[3].wait()
    loads[2].wait()
    for c in range(lz):
        put(out_h.at[c], out_l.at[c], slice(None), span(0), gate(0, c) * coup_ref[0, 0, 0, c])
        put(out_h.at[c], out_l.at[c], slice(None), span(1), gate(1, c) * coup_ref[1, 0, 0, c])
        if c + 1 == lz:
            put(zo_h, zo_l, slice(None), slice(None), gate(2, c) * coup_ref[2, 0, 0, c])
    carry(0, first_parts)
    pl.semaphore_wait(barrier, sum(extent(group, sizes) - 1 for group in COARSE_GROUPS))
    start(halo_copies(0))

    loads[1].wait()
    square_row = lax.broadcasted_iota(jnp.int32, (block, block), 0)
    square_col = lax.broadcasted_iota(jnp.int32, (block, block), 1)
    shift = jnp.where(square_row == square_col, SHIFT, 0.0)
    if lz > 2:
        loc_h[...] = jnp.zeros_like(loc_h)
        loc_l[...] = jnp.zeros_like(loc_l)
    for c in range(lz):
        put(loc_h, loc_l, span(c), span(c), diag_ref[0, 0, c] - shift)
        cx = gate(0, c) * coup_ref[0, 0, 0, c]
        cy = gate(1, c) * coup_ref[1, 0, 0, c]
        cz = gate(2, c) * coup_ref[2, 0, 0, c]
        put(in_h.at[c], in_l.at[c], span(0), slice(None), cx.T)
        put(in_h.at[c], in_l.at[c], span(1), slice(None), cy.T)
        if c + 1 < lz:
            put(loc_h, loc_l, span(c), span(c + 1), cz)
            put(loc_h, loc_l, span(c + 1), span(c), cz.T)
        else:
            put(zi_h, zi_l, slice(None), slice(None), cz.T)
    row_of = lax.broadcasted_iota(jnp.int32, (rows, wide), 0)
    own = times(first_parts, loc_h[...], loc_l[...]) + jnp.where(row_of < defl, SHIFT * first, 0.0)

    reps = block // defl
    apart = defl // reps
    lane = lax.broadcasted_iota(jnp.int32, (apart, block), 1)
    lane_row = lax.broadcasted_iota(jnp.int32, (1, block), 1)
    col = lax.broadcasted_iota(jnp.int32, (defl, block), 1)
    row = lax.broadcasted_iota(jnp.int32, (defl, block), 0)
    eye = jnp.where(row == col, 1.0, 0.0)

    def project(*below):
        held = sum(v.shape[0] for v in below)
        pads = [jnp.zeros((block - held, wide), F32)]
        put(proj_h, proj_l, slice(None), slice(None), jnp.concatenate([below[0][:defl]] * reps + list(below) + pads, axis=0))

    def pack(repeated):
        packed = jnp.zeros((apart, block), F32)
        for g in range(reps):
            inside = (lane >= g * defl) & (lane < (g + 1) * defl)
            packed = packed + jnp.where(inside, repeated[g * apart : (g + 1) * apart], 0.0)
        return packed

    def unpack(packed):
        groups = [packed] + [pltpu.roll(packed, block - g * defl, 1) for g in range(1, reps)]
        return jnp.where(col < defl, jnp.concatenate(groups, axis=0), 0.0)

    def moments(left, right_parts):
        out_a = times_t(left, proj_h[...], proj_l[...])
        out_b = times_t(right_parts, proj_h[...], proj_l[...])
        vectors = [out[defl : defl + 1, span(1)] for out in (out_a, out_b)]
        return jnp.concatenate([pack(out_a[:defl, span(0)]), pack(out_b[:defl, span(0)])] + vectors, axis=0)

    value = own + from_above(0) + from_below(0)
    chain = [first, value]
    before = first_parts
    for k in range(1, n_ops):
        keep(k, value)
        start(halo_copies(k, slice(0, 3)))
        parts = split_rows(value)
        carry(k, parts)
        start(halo_copies(k, slice(3, 6)))
        if k == 1:
            project(value, first)
        else:
            project(value)
        moments_start(k - 1, moments(before, parts))
        own = times(parts, loc_h[...], loc_l[...])
        for j in range(k - 1):
            stage = k - 1 - j
            if stage < stages:
                moments_next(j, stage)
        if k < ITERS:
            value = own + from_above(k) + from_below(k)
            chain.append(value)
            before = parts
    above = from_above(ITERS)
    half = split_rows((own + 2.0 * above)[:defl])
    peak = pack(times_t(half, proj_h[:block], proj_l[:block]))
    sem = ITERS * stages
    reduce_start(final_bufs[0], final_groups[0], sem, peak)

    e_and_n = moments_done(0)
    coarse = unpack(e_and_n[:apart])
    square = jnp.concatenate([coarse, jnp.zeros((block - defl, block), F32)], axis=0)
    inv = 0.5 * (coarse + square.T[:defl])

    def eliminate(inv, k):
        pivot = 1.0 / inv[k : k + 1, k : k + 1]
        line = jnp.where(col[:1] == k, pivot, inv[k : k + 1] * pivot)
        return jnp.where(row == k, line, jnp.where(col == k, 0.0, inv) - inv[:, k : k + 1] * line)

    pending = [(j, k - j) for k in range(n_ops - 1, n_ops - 1 + stages) for j in range(ITERS) if 0 < k - j < stages and k > n_ops - 2]
    for k in range(defl):
        if k == GJ_FIRST:
            for j, stage in pending:
                moments_next(j, stage)
        inv = eliminate(inv, k)

    lasts = [e_and_n] + [moments_done(j) for j in range(1, ITERS)]
    grams, heads, tails = [], [], []
    for j in range(ITERS):
        packs = [lasts[j][apart : 2 * apart]] if j == 0 else [lasts[j][:apart], lasts[j][apart : 2 * apart]]
        grams += [unpack(p) for p in packs]
        for i in range(2):
            line = lasts[j][2 * apart + i : 2 * apart + i + 1]
            heads.append(jnp.where(lane_row < defl, line, 0.0))
            tails.append(jnp.where(lane_row == defl, line, 0.0))
    start_row = pltpu.roll(lasts[0][2 * apart : 2 * apart + 1], block - rows, 1)
    tails = [jnp.where(lane_row == defl, start_row, 0.0)] + tails
    start_row = jnp.where(lane_row < defl, start_row, 0.0)

    def as_row(c):
        return jnp.sum(eye * c, axis=0, keepdims=True)

    def on(k, c):
        return jnp.sum(grams[k] * c, axis=0, keepdims=True)

    def solve(g):
        return jnp.sum(inv * g, axis=1, keepdims=True)

    def total(line):
        return jnp.sum(line, axis=1, keepdims=True)

    def plus(a, b):
        return b if a is None else a + b

    def spread(c, fields):
        return jnp.sum(c * fields, axis=0, keepdims=True)

    def combine(with_w, with_b, with_h):
        out = None
        if with_w is not None:
            out = spread(with_w, chain[0][:defl])
        for k, c in enumerate(with_b):
            out = plus(out, c * chain[k][defl : defl + 1])
        for k, c in enumerate(with_h):
            out = plus(out, spread(c, chain[k + 1][:defl]))
        return out

    coef = solve(start_row)
    x_w, x_b, x_h = coef, [], []
    rho, rem = [jnp.ones((1, 1), F32)], [-coef]
    dir_w = dir_b = dir_h = curv = norm = None
    for it in range(ITERS):
        deg = it + 1
        rem_rows = [as_row(c) for c in rem]
        grad = None
        for k in range(deg):
            grad = plus(grad, rho[k] * heads[k] + on(k, rem[k]))
        sums = []
        for s in range(2):
            line = None
            for i in range(deg):
                part = None
                for j in range(deg):
                    part = plus(part, 2.0 * rho[j] * heads[i + j + s])
                    line = plus(line, rho[i] * rho[j] * tails[i + j + s])
                if 2 * i + s < len(grams):
                    part = part + on(2 * i + s, rem[i])
                for j in range(i + 1, deg):
                    part = part + 2.0 * on(i + j + s, rem[j])
                line = plus(line, rem_rows[i] * part)
            sums.append(total(line))
        coef = solve(grad)
        energy = total(grad * as_row(coef))
        norm_new = sums[0]
        cross = sums[1] + SHIFT * norm_new
        if it == 0:
            dir_w, dir_b, dir_h = -coef, list(rho), list(rem)
            curv = cross - energy
        else:
            growth = norm_new / norm
            curv = cross - growth * growth * curv - energy
            dir_w = growth * dir_w - coef
            dir_b = [rho[k] + growth * dir_b[k] if k < it else rho[k] for k in range(deg)]
            dir_h = [rem[k] + growth * dir_h[k] if k < it else rem[k] for k in range(deg)]
        norm = norm_new
        img_b = [SHIFT * dir_b[0]] + [dir_b[k - 1] + SHIFT * dir_b[k] for k in range(1, deg)] + [dir_b[-1]]
        img_h = [dir_w + SHIFT * dir_h[0]] + [dir_h[k - 1] + SHIFT * dir_h[k] for k in range(1, deg)] + [dir_h[-1]]
        if it + 1 < ITERS:
            step = norm / curv
            x_w = x_w + step * dir_w
            x_b = [x_b[k] + step * dir_b[k] if k < it else step * dir_b[k] for k in range(deg)]
            x_h = [x_h[k] + step * dir_h[k] if k < it else step * dir_h[k] for k in range(deg)]
            rho = [rho[k] - step * img_b[k] if k < deg else -step * img_b[k] for k in range(deg + 1)]
            rem = [rem[k] - step * img_h[k] if k < deg else -step * img_h[k] for k in range(deg + 1)]
    chain.append(own + above + from_below(ITERS))
    top = rem[-1]
    top_row = as_row(top)
    for g in range(1, reps):
        top_row = top_row + pltpu.roll(as_row(top), g * defl, 1)
    weight = pack(top * top_row)
    x = combine(x_w, x_b, x_h)
    d = combine(dir_w, dir_b, dir_h)
    r = combine(None, rho, rem)
    s = combine(None, img_b, img_h)
    for j in range(1, len(final_groups)):
        peak = reduce_done(final_bufs[j - 1], sem)
        sem += 1
        reduce_start(final_bufs[j], final_groups[j], sem, peak)
    peak = reduce_done(final_bufs[-1], sem)
    curv = curv + total(jnp.sum(peak * weight, axis=0, keepdims=True))
    step = norm / curv
    x = x + step * d
    r = r - step * s
    for c in range(lz):
        sol_ref[0, 0, c : c + 1, :] = x[:, span(c)]
        res_ref[0, 0, c : c + 1, :] = r[:, span(c)]

    for k in range(n_ops):
        for sends, _, copy in halo_copies(k):
            pl.when(sends)(copy.wait_send)
    every = [buf for bufs in moment_bufs for buf in bufs] + list(final_bufs)
    for k, buf in enumerate(every):
        gathered(buf, red_send.at[k]).wait()


def hand_out(sol_ref, res_ref, sol_out, res_out, sol_held, res_held, sems):
    def move(routes, k):
        copies = [pltpu.make_async_copy(src, dst, sems.at[k, j]) for j, (src, dst) in enumerate(routes)]
        for copy in copies:
            copy.start()
        for copy in copies:
            copy.wait()

    move(((sol_ref, sol_held), (res_ref, res_held)), 0)
    move(((sol_held, sol_out), (res_held, res_out)), 1)


def solution(mesh):
    sizes = dict(mesh.shape)
    in_specs = (
        P("gx", "gy", "gz", None),
        P("gx", "gy", "gz", None, None),
        P(None, "gx", "gy", "gz", None, None),
        P(None, "gx", "gy", "gz"),
        P("gx", "gy", "gz", None, None),
    )
    out_specs = (P("gx", "gy", "gz", None), P("gx", "gy", "gz", None))

    def per_device(right_side, diag_blocks, couplings, pattern, deflation):
        lx, ly, lz, block = right_side.shape
        pattern = jnp.transpose(pattern, (1, 2, 3, 0))
        assert lx == 1 and ly == 1
        defl = deflation.shape[3]
        rows_first = (defl + 1 + 7) // 8 * 8
        wide = lz * block
        scratch = []
        for shape in (
            (wide, wide),
            (lz, block, 2 * block),
            (lz, 2 * block, block),
            (block, block),
            (block, block),
            (2 * block, wide),
        ):
            scratch += [pltpu.VMEM(shape, BF16)] * 2
        for _ in range(1 + ITERS):
            layer, face = (lz, rows_first, block), (rows_first, block)
            scratch += [pltpu.VMEM(layer, F32)] * 3 + [pltpu.VMEM(face, F32)]
            scratch += [pltpu.VMEM(layer, F32)] * 2 + [pltpu.VMEM(face, F32)]
            scratch += [pltpu.VMEM(layer, F32)] * 2 + [pltpu.VMEM(face, F32)]
        for _ in range(ITERS):
            for group in COARSE_GROUPS:
                scratch.append(pltpu.VMEM((extent(group, sizes), 2 * defl * defl // block + 2, block), F32))
        for group in last_groups(sizes):
            scratch.append(pltpu.VMEM((extent(group, sizes), defl * defl // block, block), F32))
        reductions = ITERS * len(COARSE_GROUPS) + len(last_groups(sizes))
        scratch += [pltpu.SemaphoreType.DMA((1 + ITERS, 6))] * 2
        scratch += [pltpu.SemaphoreType.DMA((reductions,))] * 2
        scratch.append(pltpu.SemaphoreType.DMA((5,)))
        for array in (right_side, diag_blocks, couplings, pattern, deflation):
            scratch.append(pltpu.VMEM(array.shape, array.dtype))
        vmem = pl.BlockSpec(memory_space=pltpu.VMEM)
        hbm = pl.BlockSpec(memory_space=pltpu.HBM)
        anywhere = pl.BlockSpec(memory_space=pl.ANY)
        out = jax.ShapeDtypeStruct(right_side.shape, F32)
        results = pl.pallas_call(
            functools.partial(kernel, sizes, lz, block, defl),
            out_shape=(out, out),
            in_specs=[hbm] * 5,
            out_specs=(vmem, vmem),
            scratch_shapes=scratch,
            compiler_params=pltpu.CompilerParams(
                collective_id=0, has_side_effects=True, vmem_limit_bytes=67_043_328
            ),
        )(right_side, diag_blocks, couplings, pattern, deflation)
        return pl.pallas_call(
            hand_out,
            out_shape=(out, out),
            in_specs=[anywhere, anywhere],
            out_specs=(hbm, hbm),
            scratch_shapes=[pltpu.VMEM(out.shape, F32)] * 2 + [pltpu.SemaphoreType.DMA((2, 2))],
            compiler_params=pltpu.CompilerParams(vmem_limit_bytes=67_043_328),
        )(*results)

    return jax.shard_map(
        per_device, mesh=mesh, in_specs=in_specs, out_specs=out_specs, check_vma=False
    )
```

time: 36.3 us -> 29.6 us (0.82)
  Pallas kernels: 35.5 us -> 28.8 us
    pallas_call x1, Pallas kernels: 34.2 us -> 27.6 us  [per_device(): pl.pallas_call(functools.partial(kernel, sizes, lz, block, defl), out_sha...]
where the time goes in v1:
time: 29.6 us; the launch traced here: 29.5 us
  Pallas kernels  28.8 us (97%)
  between operations  0.64 us (2%)
    pallas_call x1, Pallas kernels, per_device(): pl.pallas_call(functools.partial(kernel, sizes, lz, block, defl), out_sha...  27.6 us
    pallas_call x1, Pallas kernels, per_device(): pl.pallas_call(hand_out, out_shape=(out, out), in_specs=[anywhere, anywhe...  1.26 us

profile of v1, /device:TPU:0, one launch (start us, length us, event | category | flops | bytes accessed | tf_op | source)
XLA Modules:
  0.0 29.5 jit_solution(13912296293362118397)
XLA Ops:
  0.6 27.6 %shard_map.68 = (f32[1,1,2,128]{3,2,1,0:T(2,128)}, f32[1,1,2,128]{3,2,1,0:T(2,128)}) custom-call(f32[1,1,2,128]{3,2,1,0:T(2,128)} %refs_0_.1, f32[1,1,2,128,128]{4,3,2,1,0:T(8,128)} %refs_1_.1, f32[3,1,1,2,128,128]{5,4,3,2,1,0:T(8,128)} %refs_2_.1, s32[1,1,2,3]{3,2,1,0:T(2,128)} %bitcast.1, f32[1,1,2,32,128]{4,3,2,1,0:T(8,128)} %refs_4_.1), custom_call_target="tpu_custom_call" | custom-call | tf_op jit(solution)/shard_map/pallas_call | solution.py:553
  28.2 1.3 %shard_map.69 = (f32[1,1,2,128]{3,2,1,0:T(2,128)}, f32[1,1,2,128]{3,2,1,0:T(2,128)}) custom-call(f32[1,1,2,128]{3,2,1,0:T(2,128)} %get-tuple-element.4.sol_ref, f32[1,1,2,128]{3,2,1,0:T(2,128)} %get-tuple-element.5.res_ref), custom_call_target="tpu_custom_call" | custom-call | tf_op jit(solution)/shard_map/pallas_call | solution.py:563

commit v2 on v1

--- a/solution.py
+++ b/solution.py
@@ -15,7 +15,6 @@
 LAST_GROUPS = (("gx", "gy", "gz"),)
 DIRECT = 64
 SHIFT = 1.45
-GJ_FIRST = 10
 MESH = pl.DeviceIdType.MESH
 F32 = jnp.float32
 BF16 = jnp.bfloat16
@@ -105,8 +104,9 @@
     final_groups = last_groups(sizes)
     final_bufs = refs[at : at + len(final_groups)]
     at += len(final_groups)
-    halo_send, halo_recv, red_send, red_recv, load_sem = refs[at : at + 5]
-    staged = refs[at + 5 : at + 10]
+    held_ref = refs[at]
+    halo_send, halo_recv, red_send, red_recv, load_sem = refs[at + 1 : at + 6]
+    staged = refs[at + 6 : at + 11]
     loads = [pltpu.make_async_copy(src, dst, load_sem.at[k]) for k, (src, dst) in enumerate(zip(inputs, staged))]
     for k in (0, 4, 3, 2, 1):
         loads[k].start()
@@ -150,13 +150,14 @@
 
     def halo_copies(k, which=slice(None)):
         field, car_x, car_y, car_z, bey_x, bey_y, bey_z, arr_x, arr_y, arr_z = ops[k]
+        live = pl.ds(0, defl + 1 if k < ITERS else defl)
         routes = (
-            ("gx", -1, field, bey_x),
-            ("gy", -1, field, bey_y),
-            ("gz", -1, field.at[0], bey_z),
-            ("gx", 1, car_x, arr_x),
-            ("gy", 1, car_y, arr_y),
-            ("gz", 1, car_z, arr_z),
+            ("gx", -1, field.at[:, live], bey_x.at[:, live]),
+            ("gy", -1, field.at[:, live], bey_y.at[:, live]),
+            ("gz", -1, field.at[0, live], bey_z.at[live]),
+            ("gx", 1, car_x.at[:, live], arr_x.at[:, live]),
+            ("gy", 1, car_y.at[:, live], arr_y.at[:, live]),
+            ("gz", 1, car_z.at[live], arr_z.at[live]),
         )
         copies = []
         for j, (axis, way, src, dst) in list(enumerate(routes))[which]:
@@ -199,7 +200,8 @@
 
     def from_above(k):
         bey_x, bey_y, bey_z = ops[k][4:7]
-        arrive(halo_copies(k, slice(0, 3)))
+        with jax.named_scope(f"wait_above{k}"):
+            arrive(halo_copies(k, slice(0, 3)))
         out = []
         for c in range(lz):
             beyond = jnp.concatenate([bey_x[c], bey_y[c]], axis=1)
@@ -211,7 +213,8 @@
 
     def from_below(k):
         arr_x, arr_y, arr_z = ops[k][7:10]
-        arrive(halo_copies(k, slice(3, 6)))
+        with jax.named_scope(f"wait_below{k}"):
+            arrive(halo_copies(k, slice(3, 6)))
         out = []
         for c in range(lz):
             part = arr_x[c] + arr_y[c]
@@ -242,8 +245,12 @@
         for_peers(group, sizes, send)
 
     def reduce_done(buf, sem):
-        gathered(buf, red_recv.at[sem]).wait()
+        with jax.named_scope(f"wait_sum{sem}"):
+            gathered(buf, red_recv.at[sem]).wait()
         return jnp.sum(buf[...], axis=0)
+
+    def spread(c, fields):
+        return jnp.sum(c * fields, axis=0, keepdims=True)
 
     def moments_start(j, value):
         reduce_start(moment_bufs[j][0], COARSE_GROUPS[0], j * stages, value)
@@ -255,23 +262,28 @@
     def moments_done(j):
         return reduce_done(moment_bufs[j][-1], (j + 1) * stages - 1)
 
-    loads[0].wait()
-    loads[4].wait()
+    with jax.named_scope("load_first"):
+        loads[0].wait()
+        loads[4].wait()
     right = jnp.concatenate([right_ref[0, 0, c : c + 1, :] for c in range(lz)], axis=1)
     basis = jnp.concatenate([defl_ref[0, 0, c] for c in range(lz)], axis=1)
     first = jnp.concatenate([basis, right, jnp.zeros((rows - defl - 1, wide), F32)], axis=0)
     keep(0, first)
     first_parts = split_rows(first)
-    loads[3].wait()
-    loads[2].wait()
+    with jax.named_scope("load_second"):
+        loads[3].wait()
+        loads[2].wait()
     for c in range(lz):
         put(out_h.at[c], out_l.at[c], slice(None), span(0), gate(0, c) * coup_ref[0, 0, 0, c])
         put(out_h.at[c], out_l.at[c], slice(None), span(1), gate(1, c) * coup_ref[1, 0, 0, c])
         if c + 1 == lz:
             put(zo_h, zo_l, slice(None), slice(None), gate(2, c) * coup_ref[2, 0, 0, c])
-    carry(0, first_parts)
-    pl.semaphore_wait(barrier, sum(extent(group, sizes) - 1 for group in COARSE_GROUPS))
-    start(halo_copies(0))
+    with jax.named_scope("barrier"):
+        pl.semaphore_wait(barrier, sum(extent(group, sizes) - 1 for group in COARSE_GROUPS))
+    start(halo_copies(0, slice(0, 3)))
+    with jax.named_scope("carry0"):
+        carry(0, first_parts)
+    start(halo_copies(0, slice(3, 6)))
 
     loads[1].wait()
     square_row = lax.broadcasted_iota(jnp.int32, (block, block), 0)
@@ -325,64 +337,80 @@
         vectors = [out[defl : defl + 1, span(1)] for out in (out_a, out_b)]
         return jnp.concatenate([pack(out_a[:defl, span(0)]), pack(out_b[:defl, span(0)])] + vectors, axis=0)
 
-    value = own + from_above(0) + from_below(0)
+    def advance(k, own):
+        return jnp.where(row_of <= defl, own + from_above(k) + from_below(k), 0.0)
+
+    value = advance(0, own)
     chain = [first, value]
     before = first_parts
     for k in range(1, n_ops):
         keep(k, value)
         start(halo_copies(k, slice(0, 3)))
-        parts = split_rows(value)
-        carry(k, parts)
+        with jax.named_scope(f"carry{k}"):
+            parts = split_rows(value)
+            carry(k, parts)
         start(halo_copies(k, slice(3, 6)))
-        if k == 1:
-            project(value, first)
-        else:
-            project(value)
-        moments_start(k - 1, moments(before, parts))
+        with jax.named_scope(f"moments{k}"):
+            if k == 1:
+                project(value, first)
+            else:
+                project(value)
+            moments_start(k - 1, moments(before, parts))
         own = times(parts, loc_h[...], loc_l[...])
         for j in range(k - 1):
             stage = k - 1 - j
             if stage < stages:
                 moments_next(j, stage)
         if k < ITERS:
-            value = own + from_above(k) + from_below(k)
+            value = advance(k, own)
             chain.append(value)
             before = parts
+    pending = [(j, n_ops - 1 - j) for j in range(ITERS) if 0 < n_ops - 1 - j < stages]
+    e_and_n = moments_done(0)
+    with jax.named_scope("invert"):
+        coarse = unpack(e_and_n[:apart])
+        square = jnp.concatenate([coarse, jnp.zeros((block - defl, block), F32)], axis=0)
+        inv = 0.5 * (coarse + square.T[:defl])
+
+        def eliminate(inv, k):
+            col_a, col_b = (jnp.broadcast_to(inv[:, j : j + 1], inv.shape) for j in (k, k + 1))
+            a, b, c, d = col_a[k : k + 1], col_b[k : k + 1], col_a[k + 1 : k + 2], col_b[k + 1 : k + 2]
+            scale = 1.0 / (a * d - b * c)
+            unit_a, unit_b = col[:1] == k, col[:1] == k + 1
+            row_a = jnp.where(unit_a, 1.0, jnp.where(unit_b, 0.0, inv[k : k + 1]))
+            row_b = jnp.where(unit_b, 1.0, jnp.where(unit_a, 0.0, inv[k + 1 : k + 2]))
+            line_a = (d * row_a - b * row_b) * scale
+            line_b = (a * row_b - c * row_a) * scale
+            rest = jnp.where((col == k) | (col == k + 1), 0.0, inv) - col_a * line_a - col_b * line_b
+            return jnp.where(row == k, line_a, jnp.where(row == k + 1, line_b, rest))
+
+        for k in range(0, defl, 2):
+            inv = eliminate(inv, k)
+        start_row = pltpu.roll(e_and_n[2 * apart : 2 * apart + 1], block - rows, 1)
+        first_coef = jnp.sum(inv * jnp.where(lane_row < defl, start_row, 0.0), axis=1, keepdims=True)
+        lead = spread(first_coef, chain[ITERS][:defl])
     above = from_above(ITERS)
-    half = split_rows((own + 2.0 * above)[:defl])
-    peak = pack(times_t(half, proj_h[:block], proj_l[:block]))
-    sem = ITERS * stages
-    reduce_start(final_bufs[0], final_groups[0], sem, peak)
-
-    e_and_n = moments_done(0)
-    coarse = unpack(e_and_n[:apart])
-    square = jnp.concatenate([coarse, jnp.zeros((block - defl, block), F32)], axis=0)
-    inv = 0.5 * (coarse + square.T[:defl])
-
-    def eliminate(inv, k):
-        pivot = 1.0 / inv[k : k + 1, k : k + 1]
-        line = jnp.where(col[:1] == k, pivot, inv[k : k + 1] * pivot)
-        return jnp.where(row == k, line, jnp.where(col == k, 0.0, inv) - inv[:, k : k + 1] * line)
-
-    pending = [(j, k - j) for k in range(n_ops - 1, n_ops - 1 + stages) for j in range(ITERS) if 0 < k - j < stages and k > n_ops - 2]
-    for k in range(defl):
-        if k == GJ_FIRST:
-            for j, stage in pending:
-                moments_next(j, stage)
-        inv = eliminate(inv, k)
-
-    lasts = [e_and_n] + [moments_done(j) for j in range(1, ITERS)]
-    grams, heads, tails = [], [], []
-    for j in range(ITERS):
-        packs = [lasts[j][apart : 2 * apart]] if j == 0 else [lasts[j][:apart], lasts[j][apart : 2 * apart]]
-        grams += [unpack(p) for p in packs]
+    with jax.named_scope("peak"):
+        peak = lead * spread(first_coef, (own + 2.0 * above)[:defl])
+        peak = sum(peak[:, span(c)] for c in range(lz))
+        sem = ITERS * stages
+        reduce_start(final_bufs[0], final_groups[0], sem, peak)
+    for j, stage in pending:
+        moments_next(j, stage)
+
+    grams, heads = [], []
+    tails = [jnp.where(lane_row == defl, start_row, 0.0)]
+
+    def fetch(j):
+        held = e_and_n if j == 0 else moments_done(j)
+        packs = [held[apart : 2 * apart]] if j == 0 else [held[:apart], held[apart : 2 * apart]]
+        grams.extend(unpack(p) for p in packs)
         for i in range(2):
-            line = lasts[j][2 * apart + i : 2 * apart + i + 1]
+            line = held[2 * apart + i : 2 * apart + i + 1]
             heads.append(jnp.where(lane_row < defl, line, 0.0))
             tails.append(jnp.where(lane_row == defl, line, 0.0))
-    start_row = pltpu.roll(lasts[0][2 * apart : 2 * apart + 1], block - rows, 1)
-    tails = [jnp.where(lane_row == defl, start_row, 0.0)] + tails
-    start_row = jnp.where(lane_row < defl, start_row, 0.0)
+
+    fetch(0)
 
     def as_row(c):
         return jnp.sum(eye * c, axis=0, keepdims=True)
@@ -398,9 +426,6 @@
 
     def plus(a, b):
         return b if a is None else a + b
-
-    def spread(c, fields):
-        return jnp.sum(c * fields, axis=0, keepdims=True)
 
     def combine(with_w, with_b, with_h):
         out = None
@@ -412,12 +437,15 @@
             out = plus(out, spread(c, chain[k + 1][:defl]))
         return out
 
-    coef = solve(start_row)
+    coef = first_coef
     x_w, x_b, x_h = coef, [], []
     rho, rem = [jnp.ones((1, 1), F32)], [-coef]
+    scale_top = jnp.ones((1, 1), F32)
     dir_w = dir_b = dir_h = curv = norm = None
     for it in range(ITERS):
         deg = it + 1
+        if it + 1 < ITERS:
+            fetch(it + 1)
         rem_rows = [as_row(c) for c in rem]
         grad = None
         for k in range(deg):
@@ -454,52 +482,49 @@
         img_h = [dir_w + SHIFT * dir_h[0]] + [dir_h[k - 1] + SHIFT * dir_h[k] for k in range(1, deg)] + [dir_h[-1]]
         if it + 1 < ITERS:
             step = norm / curv
+            scale_top = scale_top * step
             x_w = x_w + step * dir_w
             x_b = [x_b[k] + step * dir_b[k] if k < it else step * dir_b[k] for k in range(deg)]
             x_h = [x_h[k] + step * dir_h[k] if k < it else step * dir_h[k] for k in range(deg)]
             rho = [rho[k] - step * img_b[k] if k < deg else -step * img_b[k] for k in range(deg + 1)]
             rem = [rem[k] - step * img_h[k] if k < deg else -step * img_h[k] for k in range(deg + 1)]
     chain.append(own + above + from_below(ITERS))
-    top = rem[-1]
-    top_row = as_row(top)
-    for g in range(1, reps):
-        top_row = top_row + pltpu.roll(as_row(top), g * defl, 1)
-    weight = pack(top * top_row)
-    x = combine(x_w, x_b, x_h)
-    d = combine(dir_w, dir_b, dir_h)
-    r = combine(None, rho, rem)
-    s = combine(None, img_b, img_h)
-    for j in range(1, len(final_groups)):
-        peak = reduce_done(final_bufs[j - 1], sem)
-        sem += 1
-        reduce_start(final_bufs[j], final_groups[j], sem, peak)
-    peak = reduce_done(final_bufs[-1], sem)
-    curv = curv + total(jnp.sum(peak * weight, axis=0, keepdims=True))
-    step = norm / curv
-    x = x + step * d
-    r = r - step * s
-    for c in range(lz):
-        sol_ref[0, 0, c : c + 1, :] = x[:, span(c)]
-        res_ref[0, 0, c : c + 1, :] = r[:, span(c)]
-
+    with jax.named_scope("combine"):
+        held_ref[0:1] = combine(x_w, x_b, x_h)
+        held_ref[1:2] = combine(dir_w, dir_b, dir_h)
+        held_ref[2:3] = combine(None, rho, rem)
+        held_ref[3:4] = combine(None, img_b, img_h)
     for k in range(n_ops):
         for sends, _, copy in halo_copies(k):
             pl.when(sends)(copy.wait_send)
     every = [buf for bufs in moment_bufs for buf in bufs] + list(final_bufs)
-    for k, buf in enumerate(every):
-        gathered(buf, red_send.at[k]).wait()
-
-
-def hand_out(sol_ref, res_ref, sol_out, res_out, sol_held, res_held, sems):
-    def move(routes, k):
-        copies = [pltpu.make_async_copy(src, dst, sems.at[k, j]) for j, (src, dst) in enumerate(routes)]
-        for copy in copies:
-            copy.start()
-        for copy in copies:
-            copy.wait()
-
-    move(((sol_ref, sol_held), (res_ref, res_held)), 0)
-    move(((sol_held, sol_out), (res_held, res_out)), 1)
+    for k, buf in enumerate(every[:-1]):
+        if k < ITERS * stages:
+            gathered(buf, red_send.at[k]).wait()
+    for j in range(1, len(final_groups)):
+        peak = reduce_done(final_bufs[j - 1], sem)
+        gathered(final_bufs[j - 1], red_send.at[sem]).wait()
+        sem += 1
+        reduce_start(final_bufs[j], final_groups[j], sem, peak)
+    peak = reduce_done(final_bufs[-1], sem)
+    with jax.named_scope("finish"):
+        curv = curv + scale_top * scale_top * total(peak)
+        step = norm / curv
+        x = held_ref[0:1] + step * held_ref[1:2]
+        r = held_ref[2:3] - step * held_ref[3:4]
+        for c in range(lz):
+            sol_ref[0, 0, c : c + 1, :] = x[:, span(c)]
+            res_ref[0, 0, c : c + 1, :] = r[:, span(c)]
+
+    gathered(every[-1], red_send.at[len(every) - 1]).wait()
+
+
+def hand_out(sol_ref, res_ref, sol_out, res_out, sems):
+    copies = [pltpu.make_async_copy(sol_ref, sol_out, sems.at[0]), pltpu.make_async_copy(res_ref, res_out, sems.at[1])]
+    for copy in copies:
+        copy.start()
+    for copy in copies:
+        copy.wait()
 
 
 def solution(mesh):
@@ -539,7 +564,8 @@
             for group in COARSE_GROUPS:
                 scratch.append(pltpu.VMEM((extent(group, sizes), 2 * defl * defl // block + 2, block), F32))
         for group in last_groups(sizes):
-            scratch.append(pltpu.VMEM((extent(group, sizes), defl * defl // block, block), F32))
+            scratch.append(pltpu.VMEM((extent(group, sizes), 1, block), F32))
+        scratch.append(pltpu.VMEM((8, wide), F32))
         reductions = ITERS * len(COARSE_GROUPS) + len(last_groups(sizes))
         scratch += [pltpu.SemaphoreType.DMA((1 + ITERS, 6))] * 2
         scratch += [pltpu.SemaphoreType.DMA((reductions,))] * 2
@@ -548,25 +574,24 @@
             scratch.append(pltpu.VMEM(array.shape, array.dtype))
         vmem = pl.BlockSpec(memory_space=pltpu.VMEM)
         hbm = pl.BlockSpec(memory_space=pltpu.HBM)
-        anywhere = pl.BlockSpec(memory_space=pl.ANY)
         out = jax.ShapeDtypeStruct(right_side.shape, F32)
         results = pl.pallas_call(
             functools.partial(kernel, sizes, lz, block, defl),
-            out_shape=(out, out),
+            out_shape=(pltpu.VMEM(out.shape, F32),) * 2,
             in_specs=[hbm] * 5,
             out_specs=(vmem, vmem),
             scratch_shapes=scratch,
             compiler_params=pltpu.CompilerParams(
-                collective_id=0, has_side_effects=True, vmem_limit_bytes=67_043_328
+                collective_id=0, has_side_effects=True, vmem_limit_bytes=67_035_136
             ),
         )(right_side, diag_blocks, couplings, pattern, deflation)
         return pl.pallas_call(
             hand_out,
             out_shape=(out, out),
-            in_specs=[anywhere, anywhere],
+            in_specs=[vmem, vmem],
             out_specs=(hbm, hbm),
-            scratch_shapes=[pltpu.VMEM(out.shape, F32)] * 2 + [pltpu.SemaphoreType.DMA((2, 2))],
-            compiler_params=pltpu.CompilerParams(vmem_limit_bytes=67_043_328),
+            scratch_shapes=[pltpu.SemaphoreType.DMA((2,))],
+            compiler_params=pltpu.CompilerParams(vmem_limit_bytes=1_048_576),
         )(*results)
 
     return jax.shard_map(

time: 29.6 us -> 25.7 us (0.87)
  Pallas kernels: 28.8 us -> 24.9 us
    pallas_call x1, Pallas kernels: 27.6 us -> 24.4 us  [per_device(): pl.pallas_call(functools.partial(kernel, sizes, lz, block, defl), out_sha...]
    pallas_call x1, Pallas kernels: 1.26 us -> 0.59 us  [per_device(): pl.pallas_call(hand_out, out_shape=(out, out), in_specs=[vmem, vmem], out...]
where the time goes in v2:
time: 25.7 us; the launch traced here: 25.6 us
  Pallas kernels  24.9 us (97%)
  between operations  0.64 us (2%)
    pallas_call x1, Pallas kernels, per_device(): pl.pallas_call(functools.partial(kernel, sizes, lz, block, defl), out_sha...  24.4 us
    pallas_call x1, Pallas kernels, per_device(): pl.pallas_call(hand_out, out_shape=(out, out), in_specs=[vmem, vmem], out...  0.59 us

profile of v2, /device:TPU:0, one launch (start us, length us, event | category | flops | bytes accessed | tf_op | source)
XLA Modules:
  0.0 25.6 jit_solution(8170823418201089294)
XLA Ops:
  0.6 24.4 %shard_map.68 = (f32[1,1,2,128]{3,2,1,0:T(2,128)S(1)}, f32[1,1,2,128]{3,2,1,0:T(2,128)S(1)}) custom-call(f32[1,1,2,128]{3,2,1,0:T(2,128)} %refs_0_.1, f32[1,1,2,128,128]{4,3,2,1,0:T(8,128)} %refs_1_.1, f32[3,1,1,2,128,128]{5,4,3,2,1,0:T(8,128)} %refs_2_.1, s32[1,1,2,3]{3,2,1,0:T(2,128)} %bitcast.1, f32[1,1,2,32,128]{4,3,2,1,0:T(8,128)} %refs_4_.1), custom_call_target="tpu_custom_call" | custom-call | tf_op jit(solution)/shard_map/pallas_call | solution.py:578
  25.0 0.6 %shard_map.69 = (f32[1,1,2,128]{3,2,1,0:T(2,128)}, f32[1,1,2,128]{3,2,1,0:T(2,128)}) custom-call(f32[1,1,2,128]{3,2,1,0:T(2,128)S(1)} %get-tuple-element.4.sol_ref, f32[1,1,2,128]{3,2,1,0:T(2,128)S(1)} %get-tuple-element.5.res_ref), custom_call_target="tpu_custom_call" | custom-call | tf_op jit(solution)/shard_map/pallas_call | solution.py:588

commit v3 on v2

--- a/solution.py
+++ b/solution.py
@@ -105,8 +105,8 @@
     final_bufs = refs[at : at + len(final_groups)]
     at += len(final_groups)
     held_ref = refs[at]
-    halo_send, halo_recv, red_send, red_recv, load_sem = refs[at + 1 : at + 6]
-    staged = refs[at + 6 : at + 11]
+    staged = refs[at + 1 : at + 6]
+    halo_send, halo_recv, red_send, red_recv, load_sem = refs[at + 6 : at + 11]
     loads = [pltpu.make_async_copy(src, dst, load_sem.at[k]) for k, (src, dst) in enumerate(zip(inputs, staged))]
     for k in (0, 4, 3, 2, 1):
         loads[k].start()
@@ -120,8 +120,19 @@
     def greet(peer):
         pl.semaphore_signal(barrier, inc=1, device_id=peer, device_id_type=MESH)
 
-    for group in COARSE_GROUPS:
-        for_peers(group, sizes, greet)
+    met = 0
+    if sizes["gy"] <= 2 and sizes["gx"] <= 4:
+        for axis in ("gx", "gy"):
+            for there, way in ((lower, -1), (upper, 1)):
+                peer = {axis: jnp.clip(idx[axis] + way, 0, sizes[axis] - 1)}
+                pl.when(there[axis])(functools.partial(greet, peer))
+                met = met + there[axis].astype(jnp.int32)
+        for_peers(("gz",), sizes, greet)
+        met = met + sizes["gz"] - 1
+    else:
+        for group in COARSE_GROUPS:
+            for_peers(group, sizes, greet)
+            met = met + extent(group, sizes) - 1
 
     def clear(axis, received, ways):
         @pl.when(jnp.logical_not(ways[axis]))
@@ -279,7 +290,7 @@
         if c + 1 == lz:
             put(zo_h, zo_l, slice(None), slice(None), gate(2, c) * coup_ref[2, 0, 0, c])
     with jax.named_scope("barrier"):
-        pl.semaphore_wait(barrier, sum(extent(group, sizes) - 1 for group in COARSE_GROUPS))
+        pl.semaphore_wait(barrier, met)
     start(halo_copies(0, slice(0, 3)))
     with jax.named_scope("carry0"):
         carry(0, first_parts)
@@ -527,6 +538,10 @@
         copy.wait()
 
 
+def scoped(body, sems, *refs):
+    pl.run_scoped(lambda *held: body(*refs, *held), *sems)
+
+
 def solution(mesh):
     sizes = dict(mesh.shape)
     in_specs = (
@@ -566,17 +581,16 @@
         for group in last_groups(sizes):
             scratch.append(pltpu.VMEM((extent(group, sizes), 1, block), F32))
         scratch.append(pltpu.VMEM((8, wide), F32))
-        reductions = ITERS * len(COARSE_GROUPS) + len(last_groups(sizes))
-        scratch += [pltpu.SemaphoreType.DMA((1 + ITERS, 6))] * 2
-        scratch += [pltpu.SemaphoreType.DMA((reductions,))] * 2
-        scratch.append(pltpu.SemaphoreType.DMA((5,)))
         for array in (right_side, diag_blocks, couplings, pattern, deflation):
             scratch.append(pltpu.VMEM(array.shape, array.dtype))
+        reductions = ITERS * len(COARSE_GROUPS) + len(last_groups(sizes))
+        halo, reds = pltpu.SemaphoreType.DMA((1 + ITERS, 6)), pltpu.SemaphoreType.DMA((reductions,))
+        sems = (halo, halo, reds, reds, pltpu.SemaphoreType.DMA((5,)))
         vmem = pl.BlockSpec(memory_space=pltpu.VMEM)
         hbm = pl.BlockSpec(memory_space=pltpu.HBM)
         out = jax.ShapeDtypeStruct(right_side.shape, F32)
         results = pl.pallas_call(
-            functools.partial(kernel, sizes, lz, block, defl),
+            functools.partial(scoped, functools.partial(kernel, sizes, lz, block, defl), sems),
             out_shape=(pltpu.VMEM(out.shape, F32),) * 2,
             in_specs=[hbm] * 5,
             out_specs=(vmem, vmem),

time: 25.7 us -> 24.2 us (0.942)
  Pallas kernels: 24.9 us -> 23.4 us
    pallas_call x1, Pallas kernels: 24.4 us -> 22.8 us  [per_device(): pl.pallas_call(functools.partial(scoped, functools.partial(kernel, sizes,...]
where the time goes in v3:
time: 24.2 us; the launch traced here: 24.1 us
  Pallas kernels  23.4 us (97%)
  between operations  0.63 us (3%)
    pallas_call x1, Pallas kernels, per_device(): pl.pallas_call(functools.partial(scoped, functools.partial(kernel, sizes,...  22.8 us
    pallas_call x1, Pallas kernels, per_device(): pl.pallas_call(hand_out, out_shape=(out, out), in_specs=[vmem, vmem], out...  0.59 us

profile of v3, /device:TPU:0, one launch (start us, length us, event | category | flops | bytes accessed | tf_op | source)
XLA Modules:
  0.0 24.1 jit_solution(17404179035593472860)
XLA Ops:
  0.6 22.8 %shard_map.68 = (f32[1,1,2,128]{3,2,1,0:T(2,128)S(1)}, f32[1,1,2,128]{3,2,1,0:T(2,128)S(1)}) custom-call(f32[1,1,2,128]{3,2,1,0:T(2,128)} %refs_0_.1, f32[1,1,2,128,128]{4,3,2,1,0:T(8,128)} %refs_1_.1, f32[3,1,1,2,128,128]{5,4,3,2,1,0:T(8,128)} %refs_2_.1, s32[1,1,2,3]{3,2,1,0:T(2,128)} %bitcast.1, f32[1,1,2,32,128]{4,3,2,1,0:T(8,128)} %refs_4_.1), custom_call_target="tpu_custom_call" | custom-call | tf_op jit(solution)/shard_map/pallas_call | solution.py:592
  23.5 0.6 %shard_map.69 = (f32[1,1,2,128]{3,2,1,0:T(2,128)}, f32[1,1,2,128]{3,2,1,0:T(2,128)}) custom-call(f32[1,1,2,128]{3,2,1,0:T(2,128)S(1)} %get-tuple-element.4.sol_ref, f32[1,1,2,128]{3,2,1,0:T(2,128)S(1)} %get-tuple-element.5.res_ref), custom_call_target="tpu_custom_call" | custom-call | tf_op jit(solution)/shard_map/pallas_call | solution.py:602

commit v4 on v3

--- a/solution.py
+++ b/solution.py
@@ -44,14 +44,15 @@
     me = position(group, sizes)
 
     def body(k, carry):
-        action(place(lax.rem(me + k, count), group, sizes))
+        index = lax.rem(me + k + 1, count)
+        action(place(index, group, sizes))
         return carry
 
     if count <= UNROLLED:
-        for k in range(1, count):
+        for k in range(count - 1):
             body(k, 0)
     else:
-        lax.fori_loop(1, count, body, 0)
+        lax.fori_loop(0, count - 1, body, 0)
 
 
 def split_rows(v):
@@ -71,10 +72,15 @@
     return high, (m - high.astype(F32)).astype(BF16)
 
 
-def times(parts, high, low):
-    out = jnp.dot(parts, high, preferred_element_type=F32)
-    out = out + jnp.dot(parts, low, preferred_element_type=F32)
+def times(parts, *matrices):
+    out = jnp.dot(parts, matrices[0], preferred_element_type=F32)
+    for matrix in matrices[1:]:
+        out = out + jnp.dot(parts, matrix, preferred_element_type=F32)
     return join_rows(out, parts.shape[0] // 3)
+
+
+def twice(parts):
+    return jnp.concatenate([parts, parts], axis=1)
 
 
 def times_t(parts, high, low):
@@ -91,13 +97,13 @@
 def kernel(sizes, lz, block, defl, *refs):
     inputs = refs[:5]
     sol_ref, res_ref = refs[5:7]
-    (loc_h, loc_l, out_h, out_l, in_h, in_l, zo_h, zo_l, zi_h, zi_l, proj_h, proj_l) = refs[7:19]
+    loc_h, loc_l, proj_h, proj_l, out_m, in_m, zo_m, zi_m = refs[7:15]
     n_ops = 1 + ITERS
-    at = 19
+    at = 15
     ops = []
     for _ in range(n_ops):
-        ops.append(refs[at : at + 10])
-        at += 10
+        ops.append(refs[at : at + 11])
+        at += 11
     stages = len(COARSE_GROUPS)
     moment_bufs = [refs[at + j * stages : at + (j + 1) * stages] for j in range(ITERS)]
     at += ITERS * stages
@@ -107,9 +113,6 @@
     held_ref = refs[at]
     staged = refs[at + 1 : at + 6]
     halo_send, halo_recv, red_send, red_recv, load_sem = refs[at + 6 : at + 11]
-    loads = [pltpu.make_async_copy(src, dst, load_sem.at[k]) for k, (src, dst) in enumerate(zip(inputs, staged))]
-    for k in (0, 4, 3, 2, 1):
-        loads[k].start()
     right_ref, diag_ref, coup_ref, pat_ref, defl_ref = staged
 
     idx = {axis: lax.axis_index(axis) for axis in AXES}
@@ -134,6 +137,10 @@
             for_peers(group, sizes, greet)
             met = met + extent(group, sizes) - 1
 
+    loads = [pltpu.make_async_copy(src, dst, load_sem.at[k]) for k, (src, dst) in enumerate(zip(inputs, staged))]
+    for k in (0, 4, 3, 2, 1):
+        loads[k].start()
+
     def clear(axis, received, ways):
         @pl.when(jnp.logical_not(ways[axis]))
         def _():
@@ -142,10 +149,10 @@
                     ref[...] = jnp.zeros_like(ref)
 
     for j, axis in enumerate(AXES):
-        clear(axis, lambda op: op[4 + j : 5 + j], upper)
-        clear(axis, lambda op: op[7 + j : 8 + j], lower)
-
-    rows = ops[0][0].shape[1]
+        clear(axis, lambda op: op[5 + j : 6 + j], upper)
+        clear(axis, lambda op: op[8 + j : 9 + j], lower)
+
+    rows = ops[0][1].shape[0]
     wide = lz * block
 
     def gate(d, c):
@@ -160,15 +167,16 @@
         return slice(c * block, (c + 1) * block)
 
     def halo_copies(k, which=slice(None)):
-        field, car_x, car_y, car_z, bey_x, bey_y, bey_z, arr_x, arr_y, arr_z = ops[k]
-        live = pl.ds(0, defl + 1 if k < ITERS else defl)
+        field, face, car_x, car_y, car_z, bey_x, bey_y, bey_z, arr_x, arr_y, arr_z = ops[k]
+        here = defl + 1 if k < ITERS else defl
+        layer, edge = pl.ds(0, lz * here), pl.ds(0, here)
         routes = (
-            ("gx", -1, field.at[:, live], bey_x.at[:, live]),
-            ("gy", -1, field.at[:, live], bey_y.at[:, live]),
-            ("gz", -1, field.at[0, live], bey_z.at[live]),
-            ("gx", 1, car_x.at[:, live], arr_x.at[:, live]),
-            ("gy", 1, car_y.at[:, live], arr_y.at[:, live]),
-            ("gz", 1, car_z.at[live], arr_z.at[live]),
+            ("gx", -1, field.at[layer], bey_x.at[layer]),
+            ("gy", -1, field.at[layer], bey_y.at[layer]),
+            ("gz", -1, face.at[edge], bey_z.at[edge]),
+            ("gx", 1, car_x.at[layer], arr_x.at[layer]),
+            ("gy", 1, car_y.at[layer], arr_y.at[layer]),
+            ("gz", 1, car_z.at[edge], arr_z.at[edge]),
         )
         copies = []
         for j, (axis, way, src, dst) in list(enumerate(routes))[which]:
@@ -196,41 +204,63 @@
         for _, comes, copy in copies:
             pl.when(comes)(copy.wait_recv)
 
+    def lay(ref, c, v):
+        ref[c * defl : (c + 1) * defl] = v[:defl]
+        ref[lz * defl + c : lz * defl + c + 1] = v[defl : defl + 1]
+
+    def lift(ref, c):
+        tail = jnp.zeros((rows - defl - 1, block), F32)
+        parts = [ref[c * defl : (c + 1) * defl], ref[lz * defl + c : lz * defl + c + 1], tail]
+        return jnp.concatenate(parts, axis=0)
+
+    def lift_face(ref):
+        tail = jnp.zeros((rows - defl - 1, block), F32)
+        return jnp.concatenate([ref[:defl], ref[defl : defl + 1], tail], axis=0)
+
     def keep(k, v):
-        field = ops[k][0]
+        field, face = ops[k][:2]
         for c in range(lz):
-            field[c] = v[:, span(c)]
+            lay(field, c, v[:, span(c)])
+        face[...] = v[:, span(0)]
 
     def carry(k, parts):
-        _, car_x, car_y, car_z = ops[k][:4]
-        for c in range(lz):
-            carried = times(parts[:, span(c)], out_h[c], out_l[c])
-            car_x[c] = carried[:, span(0)]
-            car_y[c] = carried[:, span(1)]
-        car_z[...] = times(parts[:, span(lz - 1)], zo_h[...], zo_l[...])
-
-    def from_above(k):
-        bey_x, bey_y, bey_z = ops[k][4:7]
+        car_x, car_y, car_z = ops[k][2:5]
+        with jax.named_scope(f"carry{k}"):
+            for c in range(lz):
+                carried = times(twice(parts[:, span(c)]), out_m[c])
+                lay(car_x, c, carried[:, span(0)])
+                lay(car_y, c, carried[:, span(1)])
+        start(halo_copies(k, slice(3, 5)))
+        with jax.named_scope(f"carry_z{k}"):
+            car_z[...] = times(twice(parts[:, span(lz - 1)]), zo_m[...])
+        start(halo_copies(k, slice(5, 6)))
+
+    def wait_above(k, which):
         with jax.named_scope(f"wait_above{k}"):
-            arrive(halo_copies(k, slice(0, 3)))
+            arrive(halo_copies(k, which))
+
+    def above_z(k):
+        return times(twice(split_rows(lift_face(ops[k][7]))), zi_m[...])
+
+    def above_xy(k, part_z):
+        bey_x, bey_y = ops[k][5:7]
         out = []
         for c in range(lz):
-            beyond = jnp.concatenate([bey_x[c], bey_y[c]], axis=1)
-            part = times(split_rows(beyond), in_h[c], in_l[c])
-            if c == lz - 1:
-                part = part + times(split_rows(bey_z[...]), zi_h[...], zi_l[...])
-            out.append(part)
+            beyond = jnp.concatenate([lift(bey_x, c), lift(bey_y, c)], axis=1)
+            part = times(split_rows(beyond), in_m[c])
+            part = part[:, span(0)] + part[:, span(1)]
+            out.append(part + part_z if c == lz - 1 else part)
         return jnp.concatenate(out, axis=1)
 
     def from_below(k):
-        arr_x, arr_y, arr_z = ops[k][7:10]
+        arr_x, arr_y, arr_z = ops[k][8:11]
         with jax.named_scope(f"wait_below{k}"):
             arrive(halo_copies(k, slice(3, 6)))
         out = []
         for c in range(lz):
-            part = arr_x[c] + arr_y[c]
+            part = lift(arr_x, c) + lift(arr_y, c)
             if c == 0:
-                part = part + arr_z[...]
+                part = part + lift_face(arr_z)
             out.append(part)
         return jnp.concatenate(out, axis=1)
 
@@ -285,16 +315,18 @@
         loads[3].wait()
         loads[2].wait()
     for c in range(lz):
-        put(out_h.at[c], out_l.at[c], slice(None), span(0), gate(0, c) * coup_ref[0, 0, 0, c])
-        put(out_h.at[c], out_l.at[c], slice(None), span(1), gate(1, c) * coup_ref[1, 0, 0, c])
+        for d in range(2):
+            high, rest = split_pair(gate(d, c) * coup_ref[d, 0, 0, c])
+            out_m[c, span(0), span(d)] = high
+            out_m[c, span(1), span(d)] = rest
         if c + 1 == lz:
-            put(zo_h, zo_l, slice(None), slice(None), gate(2, c) * coup_ref[2, 0, 0, c])
+            high, rest = split_pair(gate(2, c) * coup_ref[2, 0, 0, c])
+            zo_m[span(0)] = high
+            zo_m[span(1)] = rest
     with jax.named_scope("barrier"):
         pl.semaphore_wait(barrier, met)
     start(halo_copies(0, slice(0, 3)))
-    with jax.named_scope("carry0"):
-        carry(0, first_parts)
-    start(halo_copies(0, slice(3, 6)))
+    carry(0, first_parts)
 
     loads[1].wait()
     square_row = lax.broadcasted_iota(jnp.int32, (block, block), 0)
@@ -305,16 +337,18 @@
         loc_l[...] = jnp.zeros_like(loc_l)
     for c in range(lz):
         put(loc_h, loc_l, span(c), span(c), diag_ref[0, 0, c] - shift)
-        cx = gate(0, c) * coup_ref[0, 0, 0, c]
-        cy = gate(1, c) * coup_ref[1, 0, 0, c]
+        for d in range(2):
+            high, rest = split_pair((gate(d, c) * coup_ref[d, 0, 0, c]).T)
+            in_m[c, span(d), span(0)] = high
+            in_m[c, span(d), span(1)] = rest
         cz = gate(2, c) * coup_ref[2, 0, 0, c]
-        put(in_h.at[c], in_l.at[c], span(0), slice(None), cx.T)
-        put(in_h.at[c], in_l.at[c], span(1), slice(None), cy.T)
         if c + 1 < lz:
             put(loc_h, loc_l, span(c), span(c + 1), cz)
             put(loc_h, loc_l, span(c + 1), span(c), cz.T)
         else:
-            put(zi_h, zi_l, slice(None), slice(None), cz.T)
+            high, rest = split_pair(cz.T)
+            zi_m[span(0)] = high
+            zi_m[span(1)] = rest
     row_of = lax.broadcasted_iota(jnp.int32, (rows, wide), 0)
     own = times(first_parts, loc_h[...], loc_l[...]) + jnp.where(row_of < defl, SHIFT * first, 0.0)
 
@@ -349,7 +383,10 @@
         return jnp.concatenate([pack(out_a[:defl, span(0)]), pack(out_b[:defl, span(0)])] + vectors, axis=0)
 
     def advance(k, own):
-        return jnp.where(row_of <= defl, own + from_above(k) + from_below(k), 0.0)
+        wait_above(k, slice(2, 3))
+        part_z = above_z(k)
+        wait_above(k, slice(0, 2))
+        return own + above_xy(k, part_z) + from_below(k)
 
     value = advance(0, own)
     chain = [first, value]
@@ -357,16 +394,15 @@
     for k in range(1, n_ops):
         keep(k, value)
         start(halo_copies(k, slice(0, 3)))
-        with jax.named_scope(f"carry{k}"):
-            parts = split_rows(value)
+        parts = split_rows(value)
+
+        if k < ITERS:
             carry(k, parts)
-        start(halo_copies(k, slice(3, 6)))
         with jax.named_scope(f"moments{k}"):
-            if k == 1:
-                project(value, first)
-            else:
-                project(value)
+            project(*((value, first) if k == 1 else (value,)))
             moments_start(k - 1, moments(before, parts))
+        if k == ITERS:
+            carry(k, parts)
         own = times(parts, loc_h[...], loc_l[...])
         for j in range(k - 1):
             stage = k - 1 - j
@@ -400,10 +436,18 @@
         start_row = pltpu.roll(e_and_n[2 * apart : 2 * apart + 1], block - rows, 1)
         first_coef = jnp.sum(inv * jnp.where(lane_row < defl, start_row, 0.0), axis=1, keepdims=True)
         lead = spread(first_coef, chain[ITERS][:defl])
-    above = from_above(ITERS)
+        inner = lead * spread(first_coef, own[:defl])
+        peak_own = sum(inner[:, span(c)] for c in range(lz))
+        car_x, car_y, car_z, bey_x, bey_y, bey_z = ops[ITERS][2:8]
+
+        def along(ref, c):
+            return spread(first_coef, ref[c * defl : (c + 1) * defl])
+
+        sides = [(bey, c, 2.0 * along(car, c)) for car, bey in ((car_x, bey_x), (car_y, bey_y)) for c in range(lz)]
+        sides.append((bey_z, 0, 2.0 * along(car_z, 0)))
+    wait_above(ITERS, slice(0, 3))
     with jax.named_scope("peak"):
-        peak = lead * spread(first_coef, (own + 2.0 * above)[:defl])
-        peak = sum(peak[:, span(c)] for c in range(lz))
+        peak = peak_own + sum(side * along(bey, c) for bey, c, side in sides)
         sem = ITERS * stages
         reduce_start(final_bufs[0], final_groups[0], sem, peak)
     for j, stage in pending:
@@ -499,7 +543,7 @@
             x_h = [x_h[k] + step * dir_h[k] if k < it else step * dir_h[k] for k in range(deg)]
             rho = [rho[k] - step * img_b[k] if k < deg else -step * img_b[k] for k in range(deg + 1)]
             rem = [rem[k] - step * img_h[k] if k < deg else -step * img_h[k] for k in range(deg + 1)]
-    chain.append(own + above + from_below(ITERS))
+    chain.append(own + above_xy(ITERS, above_z(ITERS)) + from_below(ITERS))
     with jax.named_scope("combine"):
         held_ref[0:1] = combine(x_w, x_b, x_h)
         held_ref[1:2] = combine(dir_w, dir_b, dir_h)
@@ -561,20 +605,14 @@
         rows_first = (defl + 1 + 7) // 8 * 8
         wide = lz * block
         scratch = []
-        for shape in (
-            (wide, wide),
-            (lz, block, 2 * block),
-            (lz, 2 * block, block),
-            (block, block),
-            (block, block),
-            (2 * block, wide),
-        ):
+        for shape in ((wide, wide), (2 * block, wide)):
             scratch += [pltpu.VMEM(shape, BF16)] * 2
+        scratch += [pltpu.VMEM((lz, 2 * block, 2 * block), BF16)] * 2 + [pltpu.VMEM((2 * block, block), BF16)] * 2
+        layer, face = ((lz * (defl + 1) + 7) // 8 * 8, block), (rows_first, block)
         for _ in range(1 + ITERS):
-            layer, face = (lz, rows_first, block), (rows_first, block)
-            scratch += [pltpu.VMEM(layer, F32)] * 3 + [pltpu.VMEM(face, F32)]
-            scratch += [pltpu.VMEM(layer, F32)] * 2 + [pltpu.VMEM(face, F32)]
-            scratch += [pltpu.VMEM(layer, F32)] * 2 + [pltpu.VMEM(face, F32)]
+            scratch += [pltpu.VMEM(layer, F32), pltpu.VMEM(face, F32)]
+            for _ in range(3):
+                scratch += [pltpu.VMEM(layer, F32)] * 2 + [pltpu.VMEM(face, F32)]
         for _ in range(ITERS):
             for group in COARSE_GROUPS:
                 scratch.append(pltpu.VMEM((extent(group, sizes), 2 * defl * defl // block + 2, block), F32))

time: 24.2 us -> 23.9 us (0.988)
  Pallas kernels: 23.4 us -> 23.1 us
    pallas_call x1, Pallas kernels: 22.8 us -> 22.5 us  [per_device(): pl.pallas_call(functools.partial(scoped, functools.partial(kernel, sizes,...]
where the time goes in v4:
time: 23.9 us; the launch traced here: 23.7 us
  Pallas kernels  23.1 us (97%)
  between operations  0.63 us (3%)
    pallas_call x1, Pallas kernels, per_device(): pl.pallas_call(functools.partial(scoped, functools.partial(kernel, sizes,...  22.5 us
    pallas_call x1, Pallas kernels, per_device(): pl.pallas_call(hand_out, out_shape=(out, out), in_specs=[vmem, vmem], out...  0.59 us

profile of v4, /device:TPU:0, one launch (start us, length us, event | category | flops | bytes accessed | tf_op | source)
XLA Modules:
  0.0 23.7 jit_solution(14035635556616438356)
XLA Ops:
  0.6 22.5 %shard_map.68 = (f32[1,1,2,128]{3,2,1,0:T(2,128)S(1)}, f32[1,1,2,128]{3,2,1,0:T(2,128)S(1)}) custom-call(f32[1,1,2,128]{3,2,1,0:T(2,128)} %refs_0_.1, f32[1,1,2,128,128]{4,3,2,1,0:T(8,128)} %refs_1_.1, f32[3,1,1,2,128,128]{5,4,3,2,1,0:T(8,128)} %refs_2_.1, s32[1,1,2,3]{3,2,1,0:T(2,128)} %bitcast.1, f32[1,1,2,32,128]{4,3,2,1,0:T(8,128)} %refs_4_.1), custom_call_target="tpu_custom_call" | custom-call | tf_op jit(solution)/shard_map/pallas_call | solution.py:630
  23.1 0.6 %shard_map.69 = (f32[1,1,2,128]{3,2,1,0:T(2,128)}, f32[1,1,2,128]{3,2,1,0:T(2,128)}) custom-call(f32[1,1,2,128]{3,2,1,0:T(2,128)S(1)} %get-tuple-element.4.sol_ref, f32[1,1,2,128]{3,2,1,0:T(2,128)S(1)} %get-tuple-element.5.res_ref), custom_call_target="tpu_custom_call" | custom-call | tf_op jit(solution)/shard_map/pallas_call | solution.py:640
